TPU v7x, 128 devices: a whole 4x4x4 slice. The times are simulated.
128 devices in a mesh: freq: 4 (over z), trace: 32 (over y, x, core).
Axes of the slice: x: 4, y: 4, z: 4, core: 2. Of those that a mesh axis runs over, the one named last changes fastest.
Arguments:
- recorded: float32 [8, 2, 2048, 4096], P(None, None, 'freq', 'trace'), may hold values from -16 to 16
- multiples: float32 [8, 2, 2048, 4096], P(None, None, 'freq', 'trace'), may hold values from -6 to 6
Outputs:
- primaries: float32 [8, 2, 2048, 4096], P(None, None, 'freq', 'trace')
- filters: float32 [8, 2, 32, 64], P(None, None, 'freq')
All inputs are finite; a program needn't handle non-finite values.
Results may differ from a plain program's by a relative error of at most 0.0001.
Values sent between devices are 32-bit elements; how exact they have to be, the bound alone decides.
No kernel may reach another device: no remote copies, remote signals or barrier semaphores. Data moves between devices by JAX's collectives and lax.ppermute only.
A program may use at most 128 MiB of HBM per device.

v0:
```python
import jax
import jax.numpy as jnp
from jax import lax
from jax.experimental import pallas as pl
from jax.experimental.pallas import tpu as pltpu
from jax.sharding import Mesh
from jax.sharding import PartitionSpec as P


FB = 64
TAPS = 64
ITERS = 3
HALF = 32
LANES = 128
AXES = ("z", "y", "x", "c")
TRACE = ("y", "x", "c")

f32 = jnp.float32
bf16 = jnp.bfloat16


def split(value):
    high = value.astype(bf16)
    return high, (value - high.astype(f32)).astype(bf16)


def mm(left, right):
    return lax.dot_general(left, right, (((1,), (0,)), ((), ())), preferred_element_type=f32)


def iota(shape, axis):
    return lax.broadcasted_iota(jnp.int32, shape, axis)


def mm_t(left, right):
    return lax.dot_general(left, right, (((1,), (1,)), ((), ())), preferred_element_type=f32)


def exact(left, right, dims):
    return lax.dot_general(
        left, right, (dims, ((), ())), precision=lax.Precision.HIGHEST,
        preferred_element_type=f32,
    )


def field_spec():
    return pl.BlockSpec((2, 2, 512, LANES), lambda s: (s, 0, 0, 0))


def edge_spec():
    return pl.BlockSpec((2, 8, HALF, LANES), lambda s: (s, 0, 0, 0))


def pack_kernel(m_ref, left_ref, right_ref):
    for shot in range(4):
        for b in range(8):
            rows = pl.ds(b * FB, FB)
            turned = jnp.concatenate(
                [m_ref[shot, 0, rows, :], m_ref[shot, 1, rows, :]], axis=0
            ).T
            left_ref[shot, b] = turned[:HALF]
            right_ref[shot, b] = turned[LANES - HALF :]


def pack(first, shots, multiples):
    shape = jax.ShapeDtypeStruct((shots, 8, HALF, LANES), f32)
    edge = pl.BlockSpec((4, 8, HALF, LANES), lambda s: (s, 0, 0, 0))
    return pl.pallas_call(
        pack_kernel,
        grid=(shots // 4,),
        in_specs=[pl.BlockSpec((4, 2, 512, LANES), lambda s: (s + first // 4, 0, 0, 0))],
        out_specs=[edge, edge],
        out_shape=[shape, shape],
        name="pack",
    )(multiples)


def edges_side(shots, is_left, edge_ref, out_ref):
    lane = iota((HALF, LANES), 1)
    home = (lane % 64 >= HALF) if is_left else (lane % 64 < HALF)
    spot = lane % HALF
    sign = jnp.where(lane < 64, 1.0, -1.0)

    def load(shot, b):
        if is_left:
            return edge_ref[shot, b]
        return jnp.concatenate(
            [edge_ref[shot, b, 1:, :], jnp.zeros((1, LANES), f32)], axis=0
        )

    def one(pair, carry):
        spots = [(pair * 2 + k, b) for k in range(2) for b in range(0, 8, 2)]
        tables = []
        for shot, b in spots:
            here, there = load(shot, b), load(shot, b + 1)
            here_turn = pltpu.roll(here, 64, 1) * sign
            there_turn = pltpu.roll(there, 64, 1) * sign
            if is_left:
                against = [there, here, there_turn, here_turn]
            else:
                against = [here, there, here_turn, there_turn]
            against = split(jnp.concatenate(against, axis=0))
            rows = split(jnp.concatenate([here, there], axis=0))
            made = (
                mm_t(rows[0], against[0]) + mm_t(rows[0], against[1]) + mm_t(rows[1], against[0])
            )
            tables.append(jnp.where(home, made[:HALF], made[HALF:]))
        for step in (1, 2, 4, 8, 16):
            fill = jnp.zeros((step, LANES), f32)
            inside = (spot >= step) if is_left else (spot < HALF - step)
            for k, table in enumerate(tables):
                if is_left:
                    moved = jnp.concatenate([fill, pltpu.roll(table, step, 1)[:-step]], axis=0)
                else:
                    moved = jnp.concatenate(
                        [pltpu.roll(table, LANES - step, 1)[step:], fill], axis=0
                    )
                tables[k] = table + jnp.where(inside, moved, 0.0)
        for (shot, b), table in zip(spots, tables):
            out_ref[shot, b] = jnp.where(home, table, 0.0)
            other = pltpu.roll(table, HALF if is_left else LANES - HALF, 1)
            out_ref[shot, b + 1] = jnp.where(home, other, 0.0)
        return carry

    lax.fori_loop(0, shots // 2, one, 0)


def edges_kernel(shots, on_ref, left_ref, right_ref, out_ref):
    @pl.when(on_ref[0] == 0)
    def _():
        out_ref[...] = jnp.zeros_like(out_ref)

    @pl.when(on_ref[0] == 1)
    def _():
        edges_side(shots, True, left_ref, out_ref)

    @pl.when(on_ref[0] == 2)
    def _():
        edges_side(shots, False, right_ref, out_ref)


def edges(on, first, last):
    shots = first.shape[0]
    return pl.pallas_call(
        lambda *refs: edges_kernel(shots, *refs),
        in_specs=[pl.BlockSpec(memory_space=pltpu.SMEM)]
        + [pl.BlockSpec(memory_space=pltpu.VMEM)] * 2,
        out_shape=jax.ShapeDtypeStruct((shots, 8, HALF, LANES), f32),
        compiler_params=pltpu.CompilerParams(vmem_limit_bytes=8 * 2**20),
        name="edges",
    )(on, first, last)


def corr_kernel(shots, m_ref, r_ref, left_ref, right_ref, out_ref, high, low, w_high, w_low, acc):
    step = pl.program_id(0)
    for b in range(16):
        rows = pl.ds(b % 8 * FB, FB)
        turned = jnp.concatenate([m_ref[b // 8, 0, rows, :], m_ref[b // 8, 1, rows, :]], axis=0).T
        for part, at in ((left_ref[b // 8, b % 8], 0), (turned, HALF), (right_ref[b // 8, b % 8], HALF + LANES)):
            part_high, part_low = split(part)
            high[b, pl.ds(at, part.shape[0]), :] = part_high
            low[b, pl.ds(at, part.shape[0]), :] = part_low
    left = iota((FB, LANES), 1) < 64
    for b in range(16):
        rows = pl.ds(b % 8 * FB, FB)
        for ref, at in ((r_ref, 0), (m_ref, LANES)):
            reals, imags = split(ref[b // 8, 0, rows, :]), split(ref[b // 8, 1, rows, :])
            for real, imag, out in ((reals[0], imags[0], w_high), (reals[1], imags[1], w_low)):
                real_turn, imag_turn = pltpu.roll(real, 64, 1), pltpu.roll(imag, 64, 1)
                pieces = (
                    jnp.where(left, real, imag_turn),
                    jnp.where(left, imag, -real_turn),
                    jnp.where(left, real_turn, imag),
                    jnp.where(left, imag_turn, -real),
                )
                for k, piece in enumerate(pieces):
                    out[b, pl.ds(k * FB, FB), pl.ds(at, LANES)] = piece
    row = iota((LANES, LANES), 0)
    inner = iota((LANES, LANES), 1) % 64
    band = row - inner
    grad_mask = (band >= 1) & (band <= 64)
    auto_mask = (band >= -31) & (band <= 32)
    tail_mask = ((band <= 95) & (inner < HALF))[96:]
    for b in range(16):
        lead = jnp.concatenate([high[b, 0:128, :], high[b, 64:192, :]], axis=1)
        rest = jnp.concatenate([low[b, 0:128, :], low[b, 64:192, :]], axis=1)
        table = mm(lead, w_high[b]) + mm(lead, w_low[b]) + mm(rest, w_high[b])
        grad, auto = table[:, :LANES], table[:, LANES:]
        for kind, part, mask, start, offset in (
            (0, grad, grad_mask, 0, 0),
            (1, auto, auto_mask, 0, HALF),
            (2, auto[96:], tail_mask, 96, HALF),
        ):
            part = jnp.where(mask, part, 0.0)
            total = None
            for g in range(part.shape[0] // 8):
                piece = pltpu.roll(part[g * 8 : g * 8 + 8], (offset - start - g * 8) % LANES, 1)
                total = piece if total is None else total + piece
            acc[kind, pl.ds(step * 16 + b, 1)] = total[None]

    @pl.when(step == shots // 2 - 1)
    def _():
        count = shots * 8
        sums = []
        for kind in range(3):
            total = acc[kind].reshape(count * 8, LANES)
            level = iota(total.shape, 0)
            for bit in (1, 2, 4):
                total = jnp.where(level // bit % 2 == 1, pltpu.roll(total, LANES - bit, 1), total)
            sums.append(jnp.sum(total.reshape(count, 8, LANES), axis=1))
        flip = ((iota((LANES, LANES), 0) + iota((LANES, LANES), 1)) % LANES == 0).astype(f32)
        flip = jnp.where(iota((LANES, LANES), 0) < 64, -flip, flip)
        auto = sums[1] + exact(sums[2], flip, ((1,), (0,)))
        for y in range(4):
            for x in range(4):
                for c in range(2):
                    place, k = number(y, x, c), (c * 4 + y) * 8
                    out_ref[place, 0:8, :] = sums[0][k : k + 8]
                    out_ref[place, 8:16, :] = auto[k : k + 8]


def corr(shots, multiples, recorded, left, right):
    return pl.pallas_call(
        lambda *refs: corr_kernel(shots, *refs),
        grid=(shots // 2,),
        in_specs=[field_spec(), field_spec(), edge_spec(), edge_spec()],
        out_specs=pl.BlockSpec((32, 16, LANES), lambda s: (0, 0, 0)),
        out_shape=jax.ShapeDtypeStruct((32, 16, LANES), f32),
        scratch_shapes=[
            pltpu.VMEM((16, 192, LANES), bf16),
            pltpu.VMEM((16, 192, LANES), bf16),
            pltpu.VMEM((16, 256, 256), bf16),
            pltpu.VMEM((16, 256, 256), bf16),
            pltpu.VMEM((3, shots * 8, 8, LANES), f32),
        ],
        compiler_params=pltpu.CompilerParams(vmem_limit_bytes=60 * 2**20),
        name="corr",
    )(multiples, recorded, left, right)


def solve_kernel(weight, z_ref, *refs):
    sums_refs, (out_ref, lags, table, vec) = refs[:4], refs[4:]
    grad_rows = jnp.concatenate([ref[0:8, :] for ref in sums_refs], axis=0)
    auto_rows = jnp.concatenate([ref[8:16, :] for ref in sums_refs], axis=0)
    turn = lambda value: pltpu.roll(value, 64, 1)
    lane = iota((TAPS, LANES), 1)
    row = iota((TAPS, LANES), 0)
    group = lane // HALF
    place = lane % HALF
    block = (place + z_ref[0] * 8) % HALF
    stacked = jnp.concatenate(
        [grad_rows, turn(grad_rows), turn(grad_rows), grad_rows], axis=0
    )
    pick = (lane == LANES - 1 - row).astype(f32)
    grad = exact(pick, stacked, ((1,), (1,)))
    lag = iota((LANES, LANES), 0) - 64
    pick = (iota((LANES, LANES), 1) == jnp.abs(lag)).astype(f32)
    stacked = jnp.concatenate(
        [auto_rows, turn(auto_rows), auto_rows, turn(auto_rows)], axis=0
    )
    made = exact(pick, stacked, ((1,), (1,)))
    odd = iota((LANES, LANES), 1) // HALF % 2 == 1
    lags[0:LANES, :] = jnp.where(odd & (lag < 0), -made, made)
    for a in range(HALF):
        part = jnp.concatenate(
            [ref[pl.ds(16 + a * 8, 8), :] for ref in sums_refs], axis=0
        )
        other = turn(part)
        turned = jnp.concatenate([part, other, part, other], axis=0).T
        table[a] = turned[:TAPS]

    flip = jnp.where(group == 3, -1.0, 1.0)
    even = group % 2 == 0

    def apply(vector):
        vec[...] = vector
        total = jnp.zeros((TAPS, LANES), f32)
        for k in range(TAPS):
            total = total + lags[64 - k : 128 - k, :] * vec[k : k + 1, :]
        low = jnp.zeros((HALF, LANES), f32)
        high = jnp.zeros((HALF, LANES), f32)
        for a in range(HALF):
            low = low + table[a, :HALF] * vec[a : a + 1, :]
            high = high + table[a, HALF:] * vec[HALF + a : HALF + a + 1, :]
        total = (total - jnp.concatenate([low, high], axis=0)) * flip
        total = total + pltpu.roll(total, LANES - HALF, 1)
        return jnp.where(even, total, pltpu.roll(total, LANES - HALF, 1))

    def bend(vector):
        before = jnp.where(place == 0, pltpu.roll(vector, 97, 1), pltpu.roll(vector, 1, 1))
        after = jnp.where(
            place == HALF - 1, pltpu.roll(vector, 31, 1), pltpu.roll(vector, 127, 1)
        )
        before = jnp.where(block == 0, 0.0, before)
        after = jnp.where(block == HALF - 1, 0.0, after)
        return 2.0 * vector - before - after

    def inner(left, right):
        return 0.5 * jnp.sum(left * right, keepdims=True)

    direction = grad
    taps = jnp.zeros_like(grad)
    norm = inner(grad, grad)
    for step in range(ITERS):
        if step > 0:
            norm_next = inner(grad, grad)
            direction = grad + (norm_next / norm) * direction
            norm = norm_next
        bent = apply(direction) + weight * bend(direction)
        length = norm / inner(direction, bent)
        taps = taps + length * direction
        grad = grad - length * bent
    pick = ((iota((TAPS, LANES), 1) % 64) == TAPS - 1 - row).astype(f32)
    made = exact(taps, pick, ((0,), (0,)))
    made = jnp.where(iota((8, LANES), 1) < 64, made[:8], made[HALF : HALF + 8])
    for k in range(8):
        out_ref[k] = made


def solve(weight, z, parts):
    return pl.pallas_call(
        lambda *refs: solve_kernel(weight, *refs),
        in_specs=[pl.BlockSpec(memory_space=pltpu.SMEM)]
        + [pl.BlockSpec(memory_space=pltpu.VMEM)] * 4,
        out_shape=jax.ShapeDtypeStruct((8, 8, LANES), f32),
        scratch_shapes=[
            pltpu.VMEM((LANES, LANES), f32),
            pltpu.VMEM((HALF, TAPS, LANES), f32),
            pltpu.VMEM((TAPS, LANES), f32),
        ],
        compiler_params=pltpu.CompilerParams(vmem_limit_bytes=8 * 2**20),
        name="solve",
    )(z, *parts)


def subtract_kernel(
    m_ref, r_ref, left_ref, right_ref, taps_ref, out_ref, taps_out_ref, lead, weights
):
    lane = iota((LANES, LANES), 1)
    for b in range(0, 16, 2):
        halo = jnp.concatenate(
            [
                right_ref[b // 8, b % 8 + 1],
                left_ref[b // 8, b % 8 + 1],
                right_ref[b // 8, b % 8],
                left_ref[b // 8, b % 8],
            ], axis=0
        ).T
        halos = split(halo)
        for odd in range(2):
            rows = pl.ds((b % 8 + odd) * FB, FB)
            field = jnp.concatenate([m_ref[b // 8, 0, rows, :], m_ref[b // 8, 1, rows, :]], axis=0)
            for k, (part, ends) in enumerate(zip(split(field), halos)):
                turned = pltpu.roll(part, 64, 1)
                if odd:
                    windows = (
                        jnp.where((lane >= 32) & (lane < 64), ends, turned),
                        jnp.where(lane < 32, ends, part),
                    )
                else:
                    windows = (
                        jnp.where(lane >= 96, ends, part),
                        jnp.where((lane >= 64) & (lane < 96), ends, turned),
                    )
                for j, window in enumerate(windows):
                    at = pl.ds(k * LANES + j * FB, FB)
                    lead[b + odd, at, pl.ds(0, LANES)] = window[:FB]
                    lead[b + odd, at, pl.ds(LANES, LANES)] = window[FB:]
    first = iota((1, LANES), 1) < 64
    masks = []
    for odd in range(2):
        spot = (iota((LANES, LANES), 0) + (96 if odd else 32)) % LANES
        band = spot - lane % 64
        masks.append((band >= 1) & (band <= 64))
    for b in range(16):
        mask, shift = masks[b % 2], (32 if b % 2 else 96)
        taps = taps_ref[b // 8, pl.ds(b % 8, 1), :]
        swapped = pltpu.roll(taps, 64, 1)
        swapped = jnp.where(first, -swapped, swapped)
        for j, line in enumerate((taps, swapped)):
            spread = jnp.broadcast_to(line, (LANES, LANES))
            spread = pltpu.roll(spread, shift, 1, stride=1, stride_axis=0)
            for k, part in enumerate(split(jnp.where(mask, spread, 0.0))):
                weights[b, pl.ds(j * LANES, LANES), pl.ds(k * LANES, LANES)] = part
    half = iota((FB, LANES), 1) < 64
    for b in range(16):
        rows = pl.ds(b % 8 * FB, FB)
        made = mm(lead[b], weights[b])
        made = (made[:LANES, :LANES] + made[LANES:, :LANES]) + (
            made[:LANES, LANES:] + made[LANES:, LANES:]
        )
        made0, made1 = made[:FB], made[FB:]
        real = jnp.where(half, made0, pltpu.roll(made1, 64, 1))
        imag = jnp.where(half, pltpu.roll(made0, 64, 1), made1)
        out_ref[b // 8, 0, rows, :] = r_ref[b // 8, 0, rows, :] - real
        out_ref[b // 8, 1, rows, :] = r_ref[b // 8, 1, rows, :] - imag
    for shot in range(2):
        taps_out_ref[shot, 0] = taps_ref[shot, :, :TAPS]
        taps_out_ref[shot, 1] = taps_ref[shot, :, TAPS:]


def subtract(multiples, recorded, left, right, taps):
    shots = multiples.shape[0]
    return pl.pallas_call(
        subtract_kernel,
        grid=(shots // 2,),
        in_specs=[
            field_spec(),
            field_spec(),
            edge_spec(),
            edge_spec(),
            pl.BlockSpec((2, 8, LANES), lambda s: (s, 0, 0)),
        ],
        out_specs=[field_spec(), pl.BlockSpec((2, 2, 8, TAPS), lambda s: (s, 0, 0, 0))],
        out_shape=[
            jax.ShapeDtypeStruct(recorded.shape, f32),
            jax.ShapeDtypeStruct((shots, 2, 8, TAPS), f32),
        ],
        scratch_shapes=[
            pltpu.VMEM((16, 256, 256), bf16),
            pltpu.VMEM((16, 256, 256), bf16),
        ],
        compiler_params=pltpu.CompilerParams(vmem_limit_bytes=60 * 2**20),
        name="subtract",
    )(multiples, recorded, left, right, taps)


def number(y, x, c):
    return (y * 4 + x) * 2 + c


def spread(value, axis, step, only=None):
    pairs = []
    for y in range(4):
        for x in range(4):
            for c in range(2):
                at = {"y": y, "x": x}
                to = dict(at)
                to[axis] = (at[axis] + step) % 4
                if only is None or only(y, x):
                    pairs.append((number(y, x, c), number(to["y"], to["x"], c)))
    return lax.ppermute(value, TRACE, pairs)


def across(value, moves):
    pairs = [
        (number(y, a, c), number(y, b, c)) for y in range(4) for a, b in moves for c in range(2)
    ]
    return lax.ppermute(value, TRACE, pairs)


def body(recorded, multiples):
    shots = multiples.shape[0]
    half = shots // 2
    y, x, c = (lax.axis_index(name) for name in TRACE)
    z = lax.axis_index("z")
    place = number(y, x, c)
    on = jnp.where(place == 0, 1, jnp.where(place == 31, 2, 0)).astype(jnp.int32)[None]
    up = [(i, i + 1) for i in range(31)]
    down = [(i + 1, i) for i in range(31)]
    first, last = pack(0, shots, multiples)
    left = lax.ppermute(last, TRACE, up)
    right = lax.ppermute(first, TRACE, down)
    ends = edges(on, first, last)

    ends = ends.reshape(2, half, 8, HALF, LANES)
    other = jnp.where(c == 0, ends[1], ends[0])
    mine = jnp.where(c == 0, ends[0], ends[1])
    mine = mine + lax.ppermute(other, TRACE, [(0, 1), (31, 30)])
    edge = lax.dynamic_index_in_dim(mine, y, 0, keepdims=False)
    for step in range(1, 4):
        sent = lax.dynamic_index_in_dim(mine, (y + step) % 4, 0, keepdims=False)
        edge = edge + spread(sent, "y", step, lambda y, x: (y, x) in ((0, 0), (3, 3)))
    edge = edge + across(edge, ((0, 2), (3, 1)))
    edge = edge + across(edge, ((0, 1), (2, 3), (3, 2), (1, 0)))
    edge = edge.transpose(1, 0, 2).reshape(8 * HALF, LANES)
    along = [[(i, (i - step) % 4) for i in range(4)] for step in range(1, 4)]

    sums = corr(shots, multiples, recorded, left, right)
    sums = lax.all_to_all(sums, TRACE, 0, 0, tiled=True).sum(axis=0)
    own = jnp.concatenate([sums, edge], axis=0)
    parts = [own] + [lax.ppermute(own, "z", pairs) for pairs in along]
    weight = 0.5 * FB * 4096
    taps = solve(weight, z[None], parts)
    taps = lax.all_to_all(taps, ("c", "y"), 0, 0, tiled=True)
    return tuple(subtract(multiples, recorded, left, right, taps))


def solution(mesh):
    finer = Mesh(mesh.devices.reshape(4, 4, 4, 2), AXES)
    placed = P(None, None, "z", TRACE)
    return jax.shard_map(
        body,
        mesh=finer,
        in_specs=(placed, placed),
        out_specs=(placed, P(None, None, "z", None)),
        check_vma=False,
    )
```

profile of v0, /device:TPU:1, one launch (start us, length us, event | category | flops | bytes accessed | tf_op | source)
XLA Modules:
  0.0 107.6 jit_solution(4346309388706217641)
XLA Ops:
  0.6 3.8 %pack.1 = (f32[8,8,32,128]{3,2,1,0:T(8,128)}, f32[8,8,32,128]{3,2,1,0:T(8,128)}) custom-call(f32[8,2,512,128]{3,2,1,0:T(8,128)} %m_ref.3), custom_call_target="tpu_custom_call" | custom-call | tf_op jit(solution)/shard_map/pack/pallas_call | solution.py:68
  4.4 0.0 copy-start
  4.4 1.2 %copy-done = f32[8,8,32,128]{3,2,1,0:T(8,128)S(1)} copy-done((f32[8,8,32,128]{3,2,1,0:T(8,128)S(1)}, f32[8,8,32,128]{3,2,1,0:T(8,128)}, u32[]{:S(2)}) %copy-start) | copy-done | bytes 1048600
  5.7 0.0 copy-start.2
  5.7 1.2 %copy-done.2 = f32[8,8,32,128]{3,2,1,0:T(8,128)S(1)} copy-done((f32[8,8,32,128]{3,2,1,0:T(8,128)S(1)}, f32[8,8,32,128]{3,2,1,0:T(8,128)}, u32[]{:S(2)}) %copy-start.2) | copy-done | bytes 1048600
  6.9 0.0 copy-start.3
  6.9 0.0 copy-start.1
  6.9 0.1 edges.1
  7.0 0.9 slice_select_fusion
  7.9 1.3 %collective-permute-start.2 = (f32[4,8,32,128]{3,2,1,0:T(8,128)}, f32[4,8,32,128]{3,2,1,0:T(8,128)}, u32[]{:S(2)}, u32[]{:S(2)}) collective-permute-start(f32[4,8,32,128]{3,2,1,0:T(8,128)} %slice_select_fusion), channel_id=1, source_target_pairs={{0,1},{31,30},{32,33},{63,62},{64,65},{95,94},{96,97},{127,126}} | collective-permute-start | bytes 1572872 | tf_op jit(solution)/shard_map/ppermute | solution.py:469
  9.2 0.0 copy-done.3
  9.2 4.7 %collective-permute-start = (f32[8,8,32,128]{3,2,1,0:T(8,128)S(1)}, f32[8,8,32,128]{3,2,1,0:T(8,128)}, u32[]{:S(2)}, u32[]{:S(2)}) collective-permute-start(f32[8,8,32,128]{3,2,1,0:T(8,128)S(1)} %copy-done.3), channel_id=1, source_target_pairs={{0,1},{1,2},{2,3},{3,4},{4,5},{5,6},{6,7},{7,8},{8,9},{9,10},{10,1... | collective-permute-start | bytes 3145736 | tf_op jit(solution)/shard_map/ppermute | solution.py:462
  13.8 0.0 copy-done.1
  13.9 6.0 %collective-permute-start.1 = (f32[8,8,32,128]{3,2,1,0:T(8,128)S(1)}, f32[8,8,32,128]{3,2,1,0:T(8,128)}, u32[]{:S(2)}, u32[]{:S(2)}) collective-permute-start(f32[8,8,32,128]{3,2,1,0:T(8,128)S(1)} %copy-done.1), channel_id=1, source_target_pairs={{1,0},{2,1},{3,2},{4,3},{5,4},{6,5},{7,6},{8,7},{9,8},{10,9},{11,1... | collective-permute-start | bytes 3145736 | tf_op jit(solution)/shard_map/ppermute | solution.py:463
  20.0 0.0 collective-permute-done.2
  20.0 1.2 %select_add_fusion = f32[4,8,32,128]{3,2,1,0:T(8,128)S(1)} fusion(f32[4,8,32,128]{3,2,1,0:T(8,128)} %collective-permute-done.2, f32[8,8,32,128]{3,2,1,0:T(8,128)S(1)} %edges.1, pred[]{:T(512)S(6)} %eq.14), kind=kLoop, calls=%fused_computation | loop fusion | flops 262144 | bytes 2097153 | tf_op jit(solution)/shard_map/add | solution.py:469
  21.2 0.0 copy-start.4
  21.2 0.8 copy-done.4
  22.0 1.3 %collective-permute-start.3 = (f32[8,32,128]{2,1,0:T(8,128)S(1)}, f32[8,32,128]{2,1,0:T(8,128)S(1)}, u32[]{:S(2)}, u32[]{:S(2)}) collective-permute-start(f32[8,32,128]{2,1,0:T(8,128)S(1)} %get-tuple-element.6), channel_id=1, source_target_pairs={{0,8},{1,9},{30,6},{31,7},{32,40},{33,41},{62,38},{63,39},{64,72},... | collective-permute-start | bytes 393224 | tf_op jit(solution)/shard_map/ppermute | solution.py:442
  23.3 1.3 %collective-permute-start.5 = (f32[8,32,128]{2,1,0:T(8,128)S(1)}, f32[8,32,128]{2,1,0:T(8,128)S(1)}, u32[]{:S(2)}, u32[]{:S(2)}) collective-permute-start(f32[8,32,128]{2,1,0:T(8,128)S(1)} %get-tuple-element.7), channel_id=1, source_target_pairs={{0,24},{1,25},{30,22},{31,23},{32,56},{33,57},{62,54},{63,55},{64,... | collective-permute-start | bytes 393224 | tf_op jit(solution)/shard_map/ppermute | solution.py:442
  24.6 1.3 %collective-permute-start.4 = (f32[8,32,128]{2,1,0:T(8,128)S(1)}, f32[8,32,128]{2,1,0:T(8,128)S(1)}, u32[]{:S(2)}, u32[]{:S(2)}) collective-permute-start(f32[8,32,128]{2,1,0:T(8,128)S(1)} %get-tuple-element.8), channel_id=1, source_target_pairs={{0,16},{1,17},{30,14},{31,15},{32,48},{33,49},{62,46},{63,47},{64,... | collective-permute-start | bytes 393224 | tf_op jit(solution)/shard_map/ppermute | solution.py:442
  25.9 4.6 %collective-permute-done.3 = f32[8,32,128]{2,1,0:T(8,128)S(1)} collective-permute-done((f32[8,32,128]{2,1,0:T(8,128)S(1)}, f32[8,32,128]{2,1,0:T(8,128)S(1)}, u32[]{:S(2)}, u32[]{:S(2)}) %collective-permute-start.3) | collective-permute-done | bytes 131104 | tf_op jit(solution)/shard_map/ppermute | solution.py:442
  30.5 0.0 collective-permute-done.5
  30.5 2.8 %collective-permute-done.4 = f32[8,32,128]{2,1,0:T(8,128)S(1)} collective-permute-done((f32[8,32,128]{2,1,0:T(8,128)S(1)}, f32[8,32,128]{2,1,0:T(8,128)S(1)}, u32[]{:S(2)}, u32[]{:S(2)}) %collective-permute-start.4) | collective-permute-done | bytes 131104 | tf_op jit(solution)/shard_map/ppermute | solution.py:442
  33.3 0.9 fusion.1
  34.2 1.3 %collective-permute-start.6 = (f32[8,32,128]{2,1,0:T(8,128)S(1)}, f32[8,32,128]{2,1,0:T(8,128)S(1)}, u32[]{:S(2)}, u32[]{:S(2)}) collective-permute-start(f32[8,32,128]{2,1,0:T(8,128)S(1)} %fusion.1), channel_id=1, source_target_pairs={{0,4},{1,5},{6,2},{7,3},{8,12},{9,13},{14,10},{15,11},{16,20},{17,... | collective-permute-start | bytes 393224 | tf_op jit(solution)/shard_map/ppermute | solution.py:449
  35.5 2.6 %collective-permute-done.6 = f32[8,32,128]{2,1,0:T(8,128)S(1)} collective-permute-done((f32[8,32,128]{2,1,0:T(8,128)S(1)}, f32[8,32,128]{2,1,0:T(8,128)S(1)}, u32[]{:S(2)}, u32[]{:S(2)}) %collective-permute-start.6) | collective-permute-done | bytes 131104 | tf_op jit(solution)/shard_map/ppermute | solution.py:449
  38.2 0.7 collective-permute-start.7
  38.9 0.0 collective-permute-done.refs_2_.left_ref
  38.9 0.0 collective-permute-done.1.refs_3_.right_ref
  38.9 11.1 %corr.1 = f32[32,16,128]{2,1,0:T(8,128)} custom-call(f32[8,2,512,128]{3,2,1,0:T(8,128)} %m_ref.3, f32[8,2,512,128]{3,2,1,0:T(8,128)} %r_ref.1, f32[8,8,32,128]{3,2,1,0:T(8,128)} %collective-permute-done.refs_2_.left_ref, f32[8,8,32,128]{3,2,1,0:T(8,128)} %collective-permute-done.1.refs_3_.right_ref), custom_call_target="tpu_custom_call" | custom-call | tf_op jit(solution)/shard_map/corr/pallas_call | solution.py:223
  50.0 12.9 %all-to-all-start = ((f32[32,16,128]{2,1,0:T(8,128)}), f32[32,16,128]{2,1,0:T(8,128)S(1)}, u32[]{:S(2)}, u32[]{:S(2)}) async-start(f32[32,16,128]{2,1,0:T(8,128)} %corr.1), calls=%async_computation | async-start | bytes 524288 | tf_op jit(solution)/shard_map/all_to_all | solution.py:480
  62.8 0.0 collective-permute-done.7
  62.9 0.1 copy.6
  63.0 8.7 %all-to-all-done = f32[32,16,128]{2,1,0:T(8,128)S(1)} async-done(((f32[32,16,128]{2,1,0:T(8,128)}), f32[32,16,128]{2,1,0:T(8,128)S(1)}, u32[]{:S(2)}, u32[]{:S(2)}) %all-to-all-start) | async-done | bytes 262176 | tf_op jit(solution)/shard_map/all_to_all | solution.py:480
  71.8 1.7 %collective-permute-start.10 = (f32[272,128]{1,0:T(8,128)S(1)}, f32[272,128]{1,0:T(8,128)S(1)}, u32[]{:S(2)}, u32[]{:S(2)}) collective-permute-start(f32[272,128]{1,0:T(8,128)S(1)} %pad_maximum_fusion.refs_1_), channel_id=1, source_target_pairs={{0,32},{32,64},{64,96},{96,0},{1,33},{33,65},{65,97},{97,1},{2,34}... | collective-permute-start | bytes 417800 | tf_op jit(solution)/shard_map/ppermute | solution.py:482
  73.5 3.3 %collective-permute-start.9 = (f32[272,128]{1,0:T(8,128)S(1)}, f32[272,128]{1,0:T(8,128)S(1)}, u32[]{:S(2)}, u32[]{:S(2)}) collective-permute-start(f32[272,128]{1,0:T(8,128)S(1)} %pad_maximum_fusion.refs_1_), channel_id=1, source_target_pairs={{0,64},{32,96},{64,0},{96,32},{1,65},{33,97},{65,1},{97,33},{2,66}... | collective-permute-start | bytes 417800 | tf_op jit(solution)/shard_map/ppermute | solution.py:482
  76.8 0.7 collective-permute-start.8
  77.5 2.0 %collective-permute-done.10.refs_4_ = f32[272,128]{1,0:T(8,128)S(1)} collective-permute-done((f32[272,128]{1,0:T(8,128)S(1)}, f32[272,128]{1,0:T(8,128)S(1)}, u32[]{:S(2)}, u32[]{:S(2)}) %collective-permute-start.10) | collective-permute-done | bytes 139296 | tf_op jit(solution)/shard_map/ppermute | solution.py:482
  79.5 3.9 %collective-permute-done.9.refs_3_ = f32[272,128]{1,0:T(8,128)S(1)} collective-permute-done((f32[272,128]{1,0:T(8,128)S(1)}, f32[272,128]{1,0:T(8,128)S(1)}, u32[]{:S(2)}, u32[]{:S(2)}) %collective-permute-start.9) | collective-permute-done | bytes 139296 | tf_op jit(solution)/shard_map/ppermute | solution.py:482
  83.4 0.0 collective-permute-done.8.refs_2_
  83.4 2.8 %solve.1 = f32[8,8,128]{2,1,0:T(8,128)S(1)} custom-call(s32[1]{0:T(128)} %bitcast.refs_0_, f32[272,128]{1,0:T(8,128)S(1)} %pad_maximum_fusion.refs_1_, f32[272,128]{1,0:T(8,128)S(1)} %collective-permute-done.8.refs_2_, f32[272,128]{1,0:T(8,128)S(1)} %collective-permute-done.9.refs_3_, f32[272,128]{1,0:T(8,128)S(1)} %collective-permute-done.10.refs_4_), custom_call_target="tpu_custom_call" | custom-call | tf_op jit(solution)/shard_map/solve/pallas_call | solution.py:321
  86.2 9.0 %all_to_all.10.taps_ref = f32[8,8,128]{2,1,0:T(8,128)} all-to-all(f32[8,8,128]{2,1,0:T(8,128)S(1)} %solve.1), channel_id=1, replica_groups=mesh['z'=4,'y'=4,'x'=4,'c'=2] {'c','y'}, dimensions={0} | all-to-all | bytes 65536 | tf_op jit(solution)/shard_map/all_to_all | solution.py:485
  95.2 12.4 %subtract.1 = (f32[8,2,512,128]{3,2,1,0:T(8,128)}, f32[8,2,8,64]{3,2,1,0:T(8,128)}) custom-call(f32[8,2,512,128]{3,2,1,0:T(8,128)} %m_ref.3, f32[8,2,512,128]{3,2,1,0:T(8,128)} %r_ref.1, f32[8,8,32,128]{3,2,1,0:T(8,128)} %collective-permute-done.refs_2_.left_ref, f32[8,8,32,128]{3,2,1,0:T(8,128)} %collective-permute-done.1.refs_3_.right_ref, ...), custom_call_target="tpu_custom_call" | custom-call | tf_op jit(solution)/shard_map/subtract/pallas_call | solution.py:404
  (5 shorter events, 0.1 us)
Async XLA Ops:
  4.4 1.2 %copy-start = (f32[8,8,32,128]{3,2,1,0:T(8,128)S(1)}, f32[8,8,32,128]{3,2,1,0:T(8,128)}, u32[]{:S(2)}) copy-start(f32[8,8,32,128]{3,2,1,0:T(8,128)} %get-tuple-element.5.refs_1_) | copy-start | bytes 3145732
  5.7 1.2 %copy-start.2 = (f32[8,8,32,128]{3,2,1,0:T(8,128)S(1)}, f32[8,8,32,128]{3,2,1,0:T(8,128)}, u32[]{:S(2)}) copy-start(f32[8,8,32,128]{3,2,1,0:T(8,128)} %get-tuple-element.4.refs_2_) | copy-start | bytes 3145732
  6.9 2.3 %copy-start.3 = (f32[8,8,32,128]{3,2,1,0:T(8,128)S(1)}, f32[8,8,32,128]{3,2,1,0:T(8,128)}, u32[]{:S(2)}) copy-start(f32[8,8,32,128]{3,2,1,0:T(8,128)} %get-tuple-element.4.refs_2_) | copy-start | bytes 3145732
  6.9 7.0 %copy-start.1 = (f32[8,8,32,128]{3,2,1,0:T(8,128)S(1)}, f32[8,8,32,128]{3,2,1,0:T(8,128)}, u32[]{:S(2)}) copy-start(f32[8,8,32,128]{3,2,1,0:T(8,128)} %get-tuple-element.5.refs_1_) | copy-start | bytes 3145732
  7.9 12.1 %collective-permute-start.2 = (f32[4,8,32,128]{3,2,1,0:T(8,128)}, f32[4,8,32,128]{3,2,1,0:T(8,128)}, u32[]{:S(2)}, u32[]{:S(2)}) collective-permute-start(f32[4,8,32,128]{3,2,1,0:T(8,128)} %slice_select_fusion), channel_id=1, source_target_pairs={{0,1},{31,30},{32,33},{63,62},{64,65},{95,94},{96,97},{127,126}} | collective-permute-start | bytes 1572872 | tf_op jit(solution)/shard_map/ppermute | solution.py:469
  9.2 29.7 %collective-permute-start = (f32[8,8,32,128]{3,2,1,0:T(8,128)S(1)}, f32[8,8,32,128]{3,2,1,0:T(8,128)}, u32[]{:S(2)}, u32[]{:S(2)}) collective-permute-start(f32[8,8,32,128]{3,2,1,0:T(8,128)S(1)} %copy-done.3), channel_id=1, source_target_pairs={{0,1},{1,2},{2,3},{3,4},{4,5},{5,6},{6,7},{7,8},{8,9},{9,10},{10,1... | collective-permute-start | bytes 3145736 | tf_op jit(solution)/shard_map/ppermute | solution.py:462
  13.9 25.0 %collective-permute-start.1 = (f32[8,8,32,128]{3,2,1,0:T(8,128)S(1)}, f32[8,8,32,128]{3,2,1,0:T(8,128)}, u32[]{:S(2)}, u32[]{:S(2)}) collective-permute-start(f32[8,8,32,128]{3,2,1,0:T(8,128)S(1)} %copy-done.1), channel_id=1, source_target_pairs={{1,0},{2,1},{3,2},{4,3},{5,4},{6,5},{7,6},{8,7},{9,8},{10,9},{11,1... | collective-permute-start | bytes 3145736 | tf_op jit(solution)/shard_map/ppermute | solution.py:463
  21.2 0.8 copy-start.4
  22.0 8.5 %collective-permute-start.3 = (f32[8,32,128]{2,1,0:T(8,128)S(1)}, f32[8,32,128]{2,1,0:T(8,128)S(1)}, u32[]{:S(2)}, u32[]{:S(2)}) collective-permute-start(f32[8,32,128]{2,1,0:T(8,128)S(1)} %get-tuple-element.6), channel_id=1, source_target_pairs={{0,8},{1,9},{30,6},{31,7},{32,40},{33,41},{62,38},{63,39},{64,72},... | collective-permute-start | bytes 393224 | tf_op jit(solution)/shard_map/ppermute | solution.py:442
  23.3 7.2 %collective-permute-start.5 = (f32[8,32,128]{2,1,0:T(8,128)S(1)}, f32[8,32,128]{2,1,0:T(8,128)S(1)}, u32[]{:S(2)}, u32[]{:S(2)}) collective-permute-start(f32[8,32,128]{2,1,0:T(8,128)S(1)} %get-tuple-element.7), channel_id=1, source_target_pairs={{0,24},{1,25},{30,22},{31,23},{32,56},{33,57},{62,54},{63,55},{64,... | collective-permute-start | bytes 393224 | tf_op jit(solution)/shard_map/ppermute | solution.py:442
  24.6 8.7 %collective-permute-start.4 = (f32[8,32,128]{2,1,0:T(8,128)S(1)}, f32[8,32,128]{2,1,0:T(8,128)S(1)}, u32[]{:S(2)}, u32[]{:S(2)}) collective-permute-start(f32[8,32,128]{2,1,0:T(8,128)S(1)} %get-tuple-element.8), channel_id=1, source_target_pairs={{0,16},{1,17},{30,14},{31,15},{32,48},{33,49},{62,46},{63,47},{64,... | collective-permute-start | bytes 393224 | tf_op jit(solution)/shard_map/ppermute | solution.py:442
  34.2 3.9 %collective-permute-start.6 = (f32[8,32,128]{2,1,0:T(8,128)S(1)}, f32[8,32,128]{2,1,0:T(8,128)S(1)}, u32[]{:S(2)}, u32[]{:S(2)}) collective-permute-start(f32[8,32,128]{2,1,0:T(8,128)S(1)} %fusion.1), channel_id=1, source_target_pairs={{0,4},{1,5},{6,2},{7,3},{8,12},{9,13},{14,10},{15,11},{16,20},{17,... | collective-permute-start | bytes 393224 | tf_op jit(solution)/shard_map/ppermute | solution.py:449
  38.2 24.7 %collective-permute-start.7 = (f32[8,32,128]{2,1,0:T(8,128)S(1)}, f32[8,32,128]{2,1,0:T(8,128)S(1)}, u32[]{:S(2)}, u32[]{:S(2)}) collective-permute-start(f32[8,32,128]{2,1,0:T(8,128)S(1)} %add.72), channel_id=1, source_target_pairs={{0,2},{1,3},{4,6},{5,7},{6,4},{7,5},{2,0},{3,1},{8,10},{9,11},{12,... | collective-permute-start | bytes 393224 | tf_op jit(solution)/shard_map/ppermute | solution.py:449
  50.0 21.7 %all-to-all-start = ((f32[32,16,128]{2,1,0:T(8,128)}), f32[32,16,128]{2,1,0:T(8,128)S(1)}, u32[]{:S(2)}, u32[]{:S(2)}) async-start(f32[32,16,128]{2,1,0:T(8,128)} %corr.1), calls=%async_computation | async-start | bytes 524288 | tf_op jit(solution)/shard_map/all_to_all | solution.py:480
  71.8 7.7 %collective-permute-start.10 = (f32[272,128]{1,0:T(8,128)S(1)}, f32[272,128]{1,0:T(8,128)S(1)}, u32[]{:S(2)}, u32[]{:S(2)}) collective-permute-start(f32[272,128]{1,0:T(8,128)S(1)} %pad_maximum_fusion.refs_1_), channel_id=1, source_target_pairs={{0,32},{32,64},{64,96},{96,0},{1,33},{33,65},{65,97},{97,1},{2,34}... | collective-permute-start | bytes 417800 | tf_op jit(solution)/shard_map/ppermute | solution.py:482
  73.5 9.9 %collective-permute-start.9 = (f32[272,128]{1,0:T(8,128)S(1)}, f32[272,128]{1,0:T(8,128)S(1)}, u32[]{:S(2)}, u32[]{:S(2)}) collective-permute-start(f32[272,128]{1,0:T(8,128)S(1)} %pad_maximum_fusion.refs_1_), channel_id=1, source_target_pairs={{0,64},{32,96},{64,0},{96,32},{1,65},{33,97},{65,1},{97,33},{2,66}... | collective-permute-start | bytes 417800 | tf_op jit(solution)/shard_map/ppermute | solution.py:482
  76.8 6.6 %collective-permute-start.8 = (f32[272,128]{1,0:T(8,128)S(1)}, f32[272,128]{1,0:T(8,128)S(1)}, u32[]{:S(2)}, u32[]{:S(2)}) collective-permute-start(f32[272,128]{1,0:T(8,128)S(1)} %pad_maximum_fusion.refs_1_), channel_id=1, source_target_pairs={{0,96},{32,0},{64,32},{96,64},{1,97},{33,1},{65,33},{97,65},{2,98}... | collective-permute-start | bytes 417800 | tf_op jit(solution)/shard_map/ppermute | solution.py:482
where the time goes:
time: 108 us
  starting transfers between devices  36.5 us (34%)
  Pallas kernels  30.2 us (28%)
  waiting for transfers between devices  24.6 us (23%)
  blocking collectives  8.97 us (8%)
  local copies, waits for them, and re-layouts  3.35 us (3%)
  other arithmetic  3.11 us (3%)
    all_to_all x1, starting transfers between devices, body(): sums = lax.all_to_all(sums, TRACE, 0, 0, tiled=True).sum(axis=0)  12.9 us
    pallas_call x1, Pallas kernels, subtract(): pl.pallas_call(subtract_kernel, grid=(shots // 2,), in_specs=[field_spec(...  12.4 us
    pallas_call x1, Pallas kernels, corr(): pl.pallas_call(lambda *refs: corr_kernel(shots, *refs), grid=(shots // 2,...  11.1 us
    all_to_all x1, blocking collectives, body(): taps = lax.all_to_all(taps, ('c', 'y'), 0, 0, tiled=True)  8.97 us
    all_to_all x1, waiting for transfers between devices, body(): sums = lax.all_to_all(sums, TRACE, 0, 0, tiled=True).sum(axis=0)  8.75 us
    ppermute x3, waiting for transfers between devices, spread(): return lax.ppermute(value, TRACE, pairs)  7.38 us
    ppermute x1, starting transfers between devices, body(): right = lax.ppermute(first, TRACE, down)  6.04 us
    ppermute x3, waiting for transfers between devices, body(): parts = [own] + [lax.ppermute(own, 'z', pairs) for pairs in along]  5.87 us
  transfers between devices with their start and end apart: 12, of which 6 were waited for; matrix products, arithmetic and copies ran while one was open for 2% of the time, Pallas kernels for 10%

commit v1 on v0

--- a/solution.py
+++ b/solution.py
@@ -75,7 +75,7 @@
     )(multiples)
 
 
-def edges_side(shots, is_left, edge_ref, out_ref):
+def edges_side(shots, turn, is_left, edge_ref, out_ref):
     lane = iota((HALF, LANES), 1)
     home = (lane % 64 >= HALF) if is_left else (lane % 64 < HALF)
     spot = lane % HALF
@@ -88,8 +88,8 @@
             [edge_ref[shot, b, 1:, :], jnp.zeros((1, LANES), f32)], axis=0
         )
 
-    def one(pair, carry):
-        spots = [(pair * 2 + k, b) for k in range(2) for b in range(0, 8, 2)]
+    def one(group, carry):
+        spots = [(group * 4 + k, b) for k in range(4) for b in range(0, 8, 2)]
         tables = []
         for shot, b in spots:
             here, there = load(shot, b), load(shot, b + 1)
@@ -117,12 +117,13 @@
                     )
                 tables[k] = table + jnp.where(inside, moved, 0.0)
         for (shot, b), table in zip(spots, tables):
-            out_ref[shot, b] = jnp.where(home, table, 0.0)
+            to = lax.rem(shot + turn, shots)
+            out_ref[to, b] = jnp.where(home, table, 0.0)
             other = pltpu.roll(table, HALF if is_left else LANES - HALF, 1)
-            out_ref[shot, b + 1] = jnp.where(home, other, 0.0)
+            out_ref[to, b + 1] = jnp.where(home, other, 0.0)
         return carry
 
-    lax.fori_loop(0, shots // 2, one, 0)
+    lax.fori_loop(0, shots // 4, one, 0)
 
 
 def edges_kernel(shots, on_ref, left_ref, right_ref, out_ref):
@@ -132,11 +133,11 @@
 
     @pl.when(on_ref[0] == 1)
     def _():
-        edges_side(shots, True, left_ref, out_ref)
+        edges_side(shots, on_ref[1], True, left_ref, out_ref)
 
     @pl.when(on_ref[0] == 2)
     def _():
-        edges_side(shots, False, right_ref, out_ref)
+        edges_side(shots, on_ref[1], False, right_ref, out_ref)
 
 
 def edges(on, first, last):
@@ -455,7 +456,8 @@
     y, x, c = (lax.axis_index(name) for name in TRACE)
     z = lax.axis_index("z")
     place = number(y, x, c)
-    on = jnp.where(place == 0, 1, jnp.where(place == 31, 2, 0)).astype(jnp.int32)[None]
+    on = jnp.where(place == 0, 1, jnp.where(place == 31, 2, 0))
+    on = jnp.stack([on, c * half]).astype(jnp.int32)
     up = [(i, i + 1) for i in range(31)]
     down = [(i + 1, i) for i in range(31)]
     first, last = pack(0, shots, multiples)
@@ -463,9 +465,7 @@
     right = lax.ppermute(first, TRACE, down)
     ends = edges(on, first, last)
 
-    ends = ends.reshape(2, half, 8, HALF, LANES)
-    other = jnp.where(c == 0, ends[1], ends[0])
-    mine = jnp.where(c == 0, ends[0], ends[1])
+    mine, other = ends[:half], ends[half:]
     mine = mine + lax.ppermute(other, TRACE, [(0, 1), (31, 30)])
     edge = lax.dynamic_index_in_dim(mine, y, 0, keepdims=False)
     for step in range(1, 4):

time: 108 us -> 109 us (level)
  waiting for transfers between devices: 24.6 us -> 25.9 us
  starting transfers between devices: 36.5 us -> 35.3 us
    ppermute x3, waiting for transfers between devices: 7.38 us -> 8.63 us  [spread(): return lax.ppermute(value, TRACE, pairs)]
    ppermute x1, starting transfers between devices: 6.04 us -> 4.86 us  [body(): right = lax.ppermute(first, TRACE, down)]
where the time goes in v1:
time: 109 us; the launch traced here: 108 us
  starting transfers between devices  35.3 us (32%)
  Pallas kernels  30.8 us (28%)
  waiting for transfers between devices  25.9 us (24%)
  blocking collectives  8.97 us (8%)
  local copies, waits for them, and re-layouts  4.21 us (4%)
  other arithmetic  2.22 us (2%)
    all_to_all x1, starting transfers between devices, body(): sums = lax.all_to_all(sums, TRACE, 0, 0, tiled=True).sum(axis=0)  13.5 us
    pallas_call x1, Pallas kernels, subtract(): pl.pallas_call(subtract_kernel, grid=(shots // 2,), in_specs=[field_spec(...  12.4 us
    pallas_call x1, Pallas kernels, corr(): pl.pallas_call(lambda *refs: corr_kernel(shots, *refs), grid=(shots // 2,...  11.1 us
    all_to_all x1, blocking collectives, body(): taps = lax.all_to_all(taps, ('c', 'y'), 0, 0, tiled=True)  8.97 us
    all_to_all x1, waiting for transfers between devices, body(): sums = lax.all_to_all(sums, TRACE, 0, 0, tiled=True).sum(axis=0)  8.75 us
    ppermute x3, waiting for transfers between devices, spread(): return lax.ppermute(value, TRACE, pairs)  8.63 us
    ppermute x3, waiting for transfers between devices, body(): parts = [own] + [lax.ppermute(own, 'z', pairs) for pairs in along]  5.87 us
    ppermute x3, starting transfers between devices, body(): parts = [own] + [lax.ppermute(own, 'z', pairs) for pairs in along]  5.74 us
  transfers between devices with their start and end apart: 12, of which 6 were waited for; matrix products, arithmetic and copies ran while one was open for 2% of the time, Pallas kernels for 10%

profile of v1, /device:TPU:1, one launch (start us, length us, event | category | flops | bytes accessed | tf_op | source)
XLA Modules:
  0.0 108.2 jit_solution(126628002207086314)
XLA Ops:
  0.6 3.8 %pack.1 = (f32[8,8,32,128]{3,2,1,0:T(8,128)}, f32[8,8,32,128]{3,2,1,0:T(8,128)}) custom-call(f32[8,2,512,128]{3,2,1,0:T(8,128)} %m_ref.3), custom_call_target="tpu_custom_call" | custom-call | tf_op jit(solution)/shard_map/pack/pallas_call | solution.py:68
  4.4 0.1 pad_add_fusion.refs_0_
  4.5 0.0 copy-start
  4.5 1.2 %copy-done = f32[8,8,32,128]{3,2,1,0:T(8,128)S(1)} copy-done((f32[8,8,32,128]{3,2,1,0:T(8,128)S(1)}, f32[8,8,32,128]{3,2,1,0:T(8,128)}, u32[]{:S(2)}) %copy-start) | copy-done | bytes 1048600
  5.7 0.0 copy-start.2
  5.7 1.2 %copy-done.2 = f32[8,8,32,128]{3,2,1,0:T(8,128)S(1)} copy-done((f32[8,8,32,128]{3,2,1,0:T(8,128)S(1)}, f32[8,8,32,128]{3,2,1,0:T(8,128)}, u32[]{:S(2)}) %copy-start.2) | copy-done | bytes 1048600
  7.0 0.0 copy-start.3
  7.0 0.0 copy-start.1
  7.0 0.6 edges.1
  7.6 0.9 slice.9
  8.5 1.3 %collective-permute-start.2 = (f32[4,8,32,128]{3,2,1,0:T(8,128)}, f32[4,8,32,128]{3,2,1,0:T(8,128)}, u32[]{:S(2)}, u32[]{:S(2)}) collective-permute-start(f32[4,8,32,128]{3,2,1,0:T(8,128)} %slice.9), channel_id=1, source_target_pairs={{0,1},{31,30},{32,33},{63,62},{64,65},{95,94},{96,97},{127,126}} | collective-permute-start | bytes 1572872 | tf_op jit(solution)/shard_map/ppermute | solution.py:469
  9.8 0.0 copy-done.3
  9.8 4.7 %collective-permute-start = (f32[8,8,32,128]{3,2,1,0:T(8,128)S(1)}, f32[8,8,32,128]{3,2,1,0:T(8,128)}, u32[]{:S(2)}, u32[]{:S(2)}) collective-permute-start(f32[8,8,32,128]{3,2,1,0:T(8,128)S(1)} %copy-done.3), channel_id=1, source_target_pairs={{0,1},{1,2},{2,3},{3,4},{4,5},{5,6},{6,7},{7,8},{8,9},{9,10},{10,1... | collective-permute-start | bytes 3145736 | tf_op jit(solution)/shard_map/ppermute | solution.py:464
  14.4 0.0 copy-done.1
  14.4 4.9 %collective-permute-start.1 = (f32[8,8,32,128]{3,2,1,0:T(8,128)S(1)}, f32[8,8,32,128]{3,2,1,0:T(8,128)}, u32[]{:S(2)}, u32[]{:S(2)}) collective-permute-start(f32[8,8,32,128]{3,2,1,0:T(8,128)S(1)} %copy-done.1), channel_id=1, source_target_pairs={{1,0},{2,1},{3,2},{4,3},{5,4},{6,5},{7,6},{8,7},{9,8},{10,9},{11,1... | collective-permute-start | bytes 3145736 | tf_op jit(solution)/shard_map/ppermute | solution.py:465
  19.4 0.0 collective-permute-done.2
  19.4 1.1 %slice_add_fusion = f32[4,8,32,128]{3,2,1,0:T(8,128)S(1)} fusion(f32[4,8,32,128]{3,2,1,0:T(8,128)} %collective-permute-done.2, f32[8,8,32,128]{3,2,1,0:T(8,128)S(1)} %edges.1), kind=kLoop, calls=%fused_computation | loop fusion | flops 131072 | bytes 1572864 | tf_op jit(solution)/shard_map/add | solution.py:469
  20.5 0.0 copy-start.4
  20.5 0.8 copy-done.4
  21.3 1.3 %collective-permute-start.3 = (f32[8,32,128]{2,1,0:T(8,128)S(1)}, f32[8,32,128]{2,1,0:T(8,128)S(1)}, u32[]{:S(2)}, u32[]{:S(2)}) collective-permute-start(f32[8,32,128]{2,1,0:T(8,128)S(1)} %get-tuple-element.6), channel_id=1, source_target_pairs={{0,8},{1,9},{30,6},{31,7},{32,40},{33,41},{62,38},{63,39},{64,72},... | collective-permute-start | bytes 393224 | tf_op jit(solution)/shard_map/ppermute | solution.py:443
  22.6 1.3 %collective-permute-start.5 = (f32[8,32,128]{2,1,0:T(8,128)S(1)}, f32[8,32,128]{2,1,0:T(8,128)S(1)}, u32[]{:S(2)}, u32[]{:S(2)}) collective-permute-start(f32[8,32,128]{2,1,0:T(8,128)S(1)} %get-tuple-element.7), channel_id=1, source_target_pairs={{0,24},{1,25},{30,22},{31,23},{32,56},{33,57},{62,54},{63,55},{64,... | collective-permute-start | bytes 393224 | tf_op jit(solution)/shard_map/ppermute | solution.py:443
  23.9 1.3 %collective-permute-start.4 = (f32[8,32,128]{2,1,0:T(8,128)S(1)}, f32[8,32,128]{2,1,0:T(8,128)S(1)}, u32[]{:S(2)}, u32[]{:S(2)}) collective-permute-start(f32[8,32,128]{2,1,0:T(8,128)S(1)} %get-tuple-element.8), channel_id=1, source_target_pairs={{0,16},{1,17},{30,14},{31,15},{32,48},{33,49},{62,46},{63,47},{64,... | collective-permute-start | bytes 393224 | tf_op jit(solution)/shard_map/ppermute | solution.py:443
  25.2 5.8 %collective-permute-done.3 = f32[8,32,128]{2,1,0:T(8,128)S(1)} collective-permute-done((f32[8,32,128]{2,1,0:T(8,128)S(1)}, f32[8,32,128]{2,1,0:T(8,128)S(1)}, u32[]{:S(2)}, u32[]{:S(2)}) %collective-permute-start.3) | collective-permute-done | bytes 131104 | tf_op jit(solution)/shard_map/ppermute | solution.py:443
  31.1 0.0 collective-permute-done.5
  31.1 2.8 %collective-permute-done.4 = f32[8,32,128]{2,1,0:T(8,128)S(1)} collective-permute-done((f32[8,32,128]{2,1,0:T(8,128)S(1)}, f32[8,32,128]{2,1,0:T(8,128)S(1)}, u32[]{:S(2)}, u32[]{:S(2)}) %collective-permute-start.4) | collective-permute-done | bytes 131104 | tf_op jit(solution)/shard_map/ppermute | solution.py:443
  33.9 0.9 fusion.1
  34.8 1.3 %collective-permute-start.6 = (f32[8,32,128]{2,1,0:T(8,128)S(1)}, f32[8,32,128]{2,1,0:T(8,128)S(1)}, u32[]{:S(2)}, u32[]{:S(2)}) collective-permute-start(f32[8,32,128]{2,1,0:T(8,128)S(1)} %fusion.1), channel_id=1, source_target_pairs={{0,4},{1,5},{6,2},{7,3},{8,12},{9,13},{14,10},{15,11},{16,20},{17,... | collective-permute-start | bytes 393224 | tf_op jit(solution)/shard_map/ppermute | solution.py:450
  36.1 2.6 %collective-permute-done.6 = f32[8,32,128]{2,1,0:T(8,128)S(1)} collective-permute-done((f32[8,32,128]{2,1,0:T(8,128)S(1)}, f32[8,32,128]{2,1,0:T(8,128)S(1)}, u32[]{:S(2)}, u32[]{:S(2)}) %collective-permute-start.6) | collective-permute-done | bytes 131104 | tf_op jit(solution)/shard_map/ppermute | solution.py:450
  38.8 0.1 collective-permute-start.7
  38.8 0.0 collective-permute-done.refs_2_.left_ref
  38.9 0.0 collective-permute-done.1.refs_3_.right_ref
  38.9 11.1 %corr.1 = f32[32,16,128]{2,1,0:T(8,128)} custom-call(f32[8,2,512,128]{3,2,1,0:T(8,128)} %m_ref.3, f32[8,2,512,128]{3,2,1,0:T(8,128)} %r_ref.1, f32[8,8,32,128]{3,2,1,0:T(8,128)} %collective-permute-done.refs_2_.left_ref, f32[8,8,32,128]{3,2,1,0:T(8,128)} %collective-permute-done.1.refs_3_.right_ref), custom_call_target="tpu_custom_call" | custom-call | tf_op jit(solution)/shard_map/corr/pallas_call | solution.py:224
  49.9 13.5 %all-to-all-start = ((f32[32,16,128]{2,1,0:T(8,128)}), f32[32,16,128]{2,1,0:T(8,128)S(1)}, u32[]{:S(2)}, u32[]{:S(2)}) async-start(f32[32,16,128]{2,1,0:T(8,128)} %corr.1), calls=%async_computation | async-start | bytes 524288 | tf_op jit(solution)/shard_map/all_to_all | solution.py:480
  63.4 0.0 collective-permute-done.7
  63.5 0.1 copy.6
  63.5 8.7 %all-to-all-done = f32[32,16,128]{2,1,0:T(8,128)S(1)} async-done(((f32[32,16,128]{2,1,0:T(8,128)}), f32[32,16,128]{2,1,0:T(8,128)S(1)}, u32[]{:S(2)}, u32[]{:S(2)}) %all-to-all-start) | async-done | bytes 262176 | tf_op jit(solution)/shard_map/all_to_all | solution.py:480
  72.3 1.7 %collective-permute-start.10 = (f32[272,128]{1,0:T(8,128)S(1)}, f32[272,128]{1,0:T(8,128)S(1)}, u32[]{:S(2)}, u32[]{:S(2)}) collective-permute-start(f32[272,128]{1,0:T(8,128)S(1)} %pad_maximum_fusion.refs_1_), channel_id=1, source_target_pairs={{0,32},{32,64},{64,96},{96,0},{1,33},{33,65},{65,97},{97,1},{2,34}... | collective-permute-start | bytes 417800 | tf_op jit(solution)/shard_map/ppermute | solution.py:482
  74.1 3.3 %collective-permute-start.9 = (f32[272,128]{1,0:T(8,128)S(1)}, f32[272,128]{1,0:T(8,128)S(1)}, u32[]{:S(2)}, u32[]{:S(2)}) collective-permute-start(f32[272,128]{1,0:T(8,128)S(1)} %pad_maximum_fusion.refs_1_), channel_id=1, source_target_pairs={{0,64},{32,96},{64,0},{96,32},{1,65},{33,97},{65,1},{97,33},{2,66}... | collective-permute-start | bytes 417800 | tf_op jit(solution)/shard_map/ppermute | solution.py:482
  77.4 0.7 collective-permute-start.8
  78.1 2.0 %collective-permute-done.10.refs_4_ = f32[272,128]{1,0:T(8,128)S(1)} collective-permute-done((f32[272,128]{1,0:T(8,128)S(1)}, f32[272,128]{1,0:T(8,128)S(1)}, u32[]{:S(2)}, u32[]{:S(2)}) %collective-permute-start.10) | collective-permute-done | bytes 139296 | tf_op jit(solution)/shard_map/ppermute | solution.py:482
  80.1 3.9 %collective-permute-done.9.refs_3_ = f32[272,128]{1,0:T(8,128)S(1)} collective-permute-done((f32[272,128]{1,0:T(8,128)S(1)}, f32[272,128]{1,0:T(8,128)S(1)}, u32[]{:S(2)}, u32[]{:S(2)}) %collective-permute-start.9) | collective-permute-done | bytes 139296 | tf_op jit(solution)/shard_map/ppermute | solution.py:482
  84.0 0.0 collective-permute-done.8.refs_2_
  84.0 2.8 %solve.1 = f32[8,8,128]{2,1,0:T(8,128)S(1)} custom-call(s32[1]{0:T(128)} %bitcast.refs_0_, f32[272,128]{1,0:T(8,128)S(1)} %pad_maximum_fusion.refs_1_, f32[272,128]{1,0:T(8,128)S(1)} %collective-permute-done.8.refs_2_, f32[272,128]{1,0:T(8,128)S(1)} %collective-permute-done.9.refs_3_, f32[272,128]{1,0:T(8,128)S(1)} %collective-permute-done.10.refs_4_), custom_call_target="tpu_custom_call" | custom-call | tf_op jit(solution)/shard_map/solve/pallas_call | solution.py:322
  86.8 9.0 %all_to_all.10.taps_ref = f32[8,8,128]{2,1,0:T(8,128)} all-to-all(f32[8,8,128]{2,1,0:T(8,128)S(1)} %solve.1), channel_id=1, replica_groups=mesh['z'=4,'y'=4,'x'=4,'c'=2] {'c','y'}, dimensions={0} | all-to-all | bytes 65536 | tf_op jit(solution)/shard_map/all_to_all | solution.py:485
  95.8 12.4 %subtract.1 = (f32[8,2,512,128]{3,2,1,0:T(8,128)}, f32[8,2,8,64]{3,2,1,0:T(8,128)}) custom-call(f32[8,2,512,128]{3,2,1,0:T(8,128)} %m_ref.3, f32[8,2,512,128]{3,2,1,0:T(8,128)} %r_ref.1, f32[8,8,32,128]{3,2,1,0:T(8,128)} %collective-permute-done.refs_2_.left_ref, f32[8,8,32,128]{3,2,1,0:T(8,128)} %collective-permute-done.1.refs_3_.right_ref, ...), custom_call_target="tpu_custom_call" | custom-call | tf_op jit(solution)/shard_map/subtract/pallas_call | solution.py:405
  (5 shorter events, 0.1 us)
Async XLA Ops:
  4.5 1.2 %copy-start = (f32[8,8,32,128]{3,2,1,0:T(8,128)S(1)}, f32[8,8,32,128]{3,2,1,0:T(8,128)}, u32[]{:S(2)}) copy-start(f32[8,8,32,128]{3,2,1,0:T(8,128)} %get-tuple-element.5.refs_1_) | copy-start | bytes 3145732
  5.7 1.2 %copy-start.2 = (f32[8,8,32,128]{3,2,1,0:T(8,128)S(1)}, f32[8,8,32,128]{3,2,1,0:T(8,128)}, u32[]{:S(2)}) copy-start(f32[8,8,32,128]{3,2,1,0:T(8,128)} %get-tuple-element.4.refs_2_) | copy-start | bytes 3145732
  7.0 2.8 %copy-start.3 = (f32[8,8,32,128]{3,2,1,0:T(8,128)S(1)}, f32[8,8,32,128]{3,2,1,0:T(8,128)}, u32[]{:S(2)}) copy-start(f32[8,8,32,128]{3,2,1,0:T(8,128)} %get-tuple-element.4.refs_2_) | copy-start | bytes 3145732
  7.0 7.5 %copy-start.1 = (f32[8,8,32,128]{3,2,1,0:T(8,128)S(1)}, f32[8,8,32,128]{3,2,1,0:T(8,128)}, u32[]{:S(2)}) copy-start(f32[8,8,32,128]{3,2,1,0:T(8,128)} %get-tuple-element.5.refs_1_) | copy-start | bytes 3145732
  8.5 10.9 %collective-permute-start.2 = (f32[4,8,32,128]{3,2,1,0:T(8,128)}, f32[4,8,32,128]{3,2,1,0:T(8,128)}, u32[]{:S(2)}, u32[]{:S(2)}) collective-permute-start(f32[4,8,32,128]{3,2,1,0:T(8,128)} %slice.9), channel_id=1, source_target_pairs={{0,1},{31,30},{32,33},{63,62},{64,65},{95,94},{96,97},{127,126}} | collective-permute-start | bytes 1572872 | tf_op jit(solution)/shard_map/ppermute | solution.py:469
  9.8 29.1 %collective-permute-start = (f32[8,8,32,128]{3,2,1,0:T(8,128)S(1)}, f32[8,8,32,128]{3,2,1,0:T(8,128)}, u32[]{:S(2)}, u32[]{:S(2)}) collective-permute-start(f32[8,8,32,128]{3,2,1,0:T(8,128)S(1)} %copy-done.3), channel_id=1, source_target_pairs={{0,1},{1,2},{2,3},{3,4},{4,5},{5,6},{6,7},{7,8},{8,9},{9,10},{10,1... | collective-permute-start | bytes 3145736 | tf_op jit(solution)/shard_map/ppermute | solution.py:464
  14.4 24.4 %collective-permute-start.1 = (f32[8,8,32,128]{3,2,1,0:T(8,128)S(1)}, f32[8,8,32,128]{3,2,1,0:T(8,128)}, u32[]{:S(2)}, u32[]{:S(2)}) collective-permute-start(f32[8,8,32,128]{3,2,1,0:T(8,128)S(1)} %copy-done.1), channel_id=1, source_target_pairs={{1,0},{2,1},{3,2},{4,3},{5,4},{6,5},{7,6},{8,7},{9,8},{10,9},{11,1... | collective-permute-start | bytes 3145736 | tf_op jit(solution)/shard_map/ppermute | solution.py:465
  20.5 0.8 copy-start.4
  21.3 9.7 %collective-permute-start.3 = (f32[8,32,128]{2,1,0:T(8,128)S(1)}, f32[8,32,128]{2,1,0:T(8,128)S(1)}, u32[]{:S(2)}, u32[]{:S(2)}) collective-permute-start(f32[8,32,128]{2,1,0:T(8,128)S(1)} %get-tuple-element.6), channel_id=1, source_target_pairs={{0,8},{1,9},{30,6},{31,7},{32,40},{33,41},{62,38},{63,39},{64,72},... | collective-permute-start | bytes 393224 | tf_op jit(solution)/shard_map/ppermute | solution.py:443
  22.6 8.4 %collective-permute-start.5 = (f32[8,32,128]{2,1,0:T(8,128)S(1)}, f32[8,32,128]{2,1,0:T(8,128)S(1)}, u32[]{:S(2)}, u32[]{:S(2)}) collective-permute-start(f32[8,32,128]{2,1,0:T(8,128)S(1)} %get-tuple-element.7), channel_id=1, source_target_pairs={{0,24},{1,25},{30,22},{31,23},{32,56},{33,57},{62,54},{63,55},{64,... | collective-permute-start | bytes 393224 | tf_op jit(solution)/shard_map/ppermute | solution.py:443
  23.9 9.9 %collective-permute-start.4 = (f32[8,32,128]{2,1,0:T(8,128)S(1)}, f32[8,32,128]{2,1,0:T(8,128)S(1)}, u32[]{:S(2)}, u32[]{:S(2)}) collective-permute-start(f32[8,32,128]{2,1,0:T(8,128)S(1)} %get-tuple-element.8), channel_id=1, source_target_pairs={{0,16},{1,17},{30,14},{31,15},{32,48},{33,49},{62,46},{63,47},{64,... | collective-permute-start | bytes 393224 | tf_op jit(solution)/shard_map/ppermute | solution.py:443
  34.8 3.9 %collective-permute-start.6 = (f32[8,32,128]{2,1,0:T(8,128)S(1)}, f32[8,32,128]{2,1,0:T(8,128)S(1)}, u32[]{:S(2)}, u32[]{:S(2)}) collective-permute-start(f32[8,32,128]{2,1,0:T(8,128)S(1)} %fusion.1), channel_id=1, source_target_pairs={{0,4},{1,5},{6,2},{7,3},{8,12},{9,13},{14,10},{15,11},{16,20},{17,... | collective-permute-start | bytes 393224 | tf_op jit(solution)/shard_map/ppermute | solution.py:450
  38.8 24.7 %collective-permute-start.7 = (f32[8,32,128]{2,1,0:T(8,128)S(1)}, f32[8,32,128]{2,1,0:T(8,128)S(1)}, u32[]{:S(2)}, u32[]{:S(2)}) collective-permute-start(f32[8,32,128]{2,1,0:T(8,128)S(1)} %add.72), channel_id=1, source_target_pairs={{0,2},{1,3},{4,6},{5,7},{6,4},{7,5},{2,0},{3,1},{8,10},{9,11},{12,... | collective-permute-start | bytes 393224 | tf_op jit(solution)/shard_map/ppermute | solution.py:450
  49.9 22.4 %all-to-all-start = ((f32[32,16,128]{2,1,0:T(8,128)}), f32[32,16,128]{2,1,0:T(8,128)S(1)}, u32[]{:S(2)}, u32[]{:S(2)}) async-start(f32[32,16,128]{2,1,0:T(8,128)} %corr.1), calls=%async_computation | async-start | bytes 524288 | tf_op jit(solution)/shard_map/all_to_all | solution.py:480
  72.3 7.7 %collective-permute-start.10 = (f32[272,128]{1,0:T(8,128)S(1)}, f32[272,128]{1,0:T(8,128)S(1)}, u32[]{:S(2)}, u32[]{:S(2)}) collective-permute-start(f32[272,128]{1,0:T(8,128)S(1)} %pad_maximum_fusion.refs_1_), channel_id=1, source_target_pairs={{0,32},{32,64},{64,96},{96,0},{1,33},{33,65},{65,97},{97,1},{2,34}... | collective-permute-start | bytes 417800 | tf_op jit(solution)/shard_map/ppermute | solution.py:482
  74.1 9.9 %collective-permute-start.9 = (f32[272,128]{1,0:T(8,128)S(1)}, f32[272,128]{1,0:T(8,128)S(1)}, u32[]{:S(2)}, u32[]{:S(2)}) collective-permute-start(f32[272,128]{1,0:T(8,128)S(1)} %pad_maximum_fusion.refs_1_), channel_id=1, source_target_pairs={{0,64},{32,96},{64,0},{96,32},{1,65},{33,97},{65,1},{97,33},{2,66}... | collective-permute-start | bytes 417800 | tf_op jit(solution)/shard_map/ppermute | solution.py:482
  77.4 6.6 %collective-permute-start.8 = (f32[272,128]{1,0:T(8,128)S(1)}, f32[272,128]{1,0:T(8,128)S(1)}, u32[]{:S(2)}, u32[]{:S(2)}) collective-permute-start(f32[272,128]{1,0:T(8,128)S(1)} %pad_maximum_fusion.refs_1_), channel_id=1, source_target_pairs={{0,96},{32,0},{64,32},{96,64},{1,97},{33,1},{65,33},{97,65},{2,98}... | collective-permute-start | bytes 417800 | tf_op jit(solution)/shard_map/ppermute | solution.py:482
